TPU v7x, 256 devices: a whole 4x4x8 slice. The times are simulated.
256 devices in a mesh: batch: 4 (over x_lo, core), seq: 64 (over y, x_hi, z).
Axes of the slice: x: 4 (x_hi: 2, x_lo: 2; x = x_hi * 2 + x_lo), y: 4, z: 8, core: 2. Of those that a mesh axis runs over, the one named last changes fastest.
Arguments:
- signal: bfloat16 [4, 16384, 256], P('batch', 'seq'), may hold values from -0.125 to 0.125
- grad_out: bfloat16 [4, 16384, 256], P('batch', 'seq'), may hold values from -6 to 6
- filter_taps: float32 [16384, 256], P('seq'), may hold values from -0.125 to 0.125
- skip_gain: float32 [256], replicated, may hold values from 0.5 to 2
Outputs:
- input_grad: bfloat16 [4, 16384, 256], P('batch', 'seq')
- filter_grad: float32 [16384, 256], P('seq')
All inputs are finite; a program needn't handle non-finite values.
Results may differ from a plain program's by a relative error of at most 0.001.
Values sent between devices are 32-bit elements; how exact they have to be, the bound alone decides.
A program may use at most 64 MiB of HBM per device.

v0:
```python
import jax
import jax.numpy as jnp
from jax import lax
from jax.sharding import PartitionSpec as P


def split_up(x, dim, devices):
    shape = x.shape
    parts = x.reshape(*shape[:dim], devices, shape[dim] // devices, *shape[dim + 1 :])
    return jnp.moveaxis(parts, dim, 0)


def summed_on_arrival(x, axis, dim):
    parts = split_up(x, dim, lax.axis_size(axis))
    arrived = lax.all_to_all(parts, axis, split_axis=0, concat_axis=0, tiled=True)
    return arrived.sum(axis=0)


def copy_for_each(x, axis):
    devices = lax.axis_size(axis)
    return lax.all_to_all(jnp.broadcast_to(x[None], (devices, *x.shape)), axis, 0, 0, tiled=True)


def in_order(parts, dim):
    shape = list(parts.shape[1:])
    shape[dim] *= parts.shape[0]
    return jnp.moveaxis(parts, 0, dim).reshape(shape)


def gather_directly(x, axis, dim):
    parts = copy_for_each(x, axis)
    return in_order(parts, dim)


def angle_table(height, width, period):
    product = lax.broadcasted_iota(jnp.int32, (height, width), 0) * lax.broadcasted_iota(
        jnp.int32, (height, width), 1
    )
    return 2.0 * jnp.pi / period * (product % period).astype(jnp.float32)


def angle_of(product, period):
    return 2.0 * jnp.pi / period * (product % period).astype(jnp.float32)


def coarse_order(slot, seq_count):
    pair_index = slot // 2
    odd_slot = slot % 2
    return jnp.where(
        pair_index == 0,
        odd_slot * seq_count,
        jnp.where(odd_slot == 0, pair_index, 2 * seq_count - pair_index),
    )


def contract(form, table, operand):
    return jnp.einsum(form, table, operand, precision=lax.Precision.HIGHEST)


def forward_spectra(columns):
    seq_count = lax.axis_size("seq")
    row_count = columns.shape[0]
    part_rows = row_count // seq_count
    period_len = 2 * row_count * seq_count
    spread = lax.all_to_all(
        columns.reshape(1, row_count, columns.shape[1]),
        "seq",
        split_axis=1,
        concat_axis=0,
        tiled=True,
    )
    slot_grid = lax.broadcasted_iota(jnp.int32, (2 * seq_count, seq_count), 0)
    source_grid = lax.broadcasted_iota(jnp.int32, (2 * seq_count, seq_count), 1)
    first_table = angle_of(coarse_order(slot_grid, seq_count) * source_grid, 2 * seq_count)
    cos_first = jnp.cos(first_table)
    sin_first = jnp.sin(first_table)
    half_width = spread.shape[2] // 2
    real_in = spread[:, :, :half_width]
    imag_in = spread[:, :, half_width:]
    real_part = contract("ks,srw->krw", cos_first, real_in) + contract(
        "ks,srw->krw", sin_first, imag_in
    )
    imag_part = contract("ks,srw->krw", cos_first, imag_in) - contract(
        "ks,srw->krw", sin_first, real_in
    )
    global_row = lax.axis_index("seq") * part_rows + lax.broadcasted_iota(
        jnp.int32, (2 * seq_count, part_rows), 1
    )
    coarse = coarse_order(lax.broadcasted_iota(jnp.int32, (2 * seq_count, part_rows), 0), seq_count)
    phases = angle_of(global_row * coarse, period_len)
    cos_turn = jnp.cos(phases)[:, :, None]
    sin_turn = jnp.sin(phases)[:, :, None]
    rotated = jnp.stack(
        [real_part * cos_turn + imag_part * sin_turn, imag_part * cos_turn - real_part * sin_turn]
    )
    inner_table = angle_table(row_count, row_count, row_count)
    cos_inner = jnp.cos(inner_table)
    sin_inner = jnp.sin(inner_table)
    pieces = lax.all_to_all(rotated, "seq", split_axis=1, concat_axis=2, tiled=True)
    real_sum = contract("qr,krw->kqw", cos_inner, pieces[0]) + contract(
        "qr,krw->kqw", sin_inner, pieces[1]
    )
    imag_sum = contract("qr,krw->kqw", cos_inner, pieces[1]) - contract(
        "qr,krw->kqw", sin_inner, pieces[0]
    )
    return jnp.stack([real_sum, imag_sum])


def split_pairs(packed):
    reversed_q = packed[:, :, ::-1]
    zero_row = jnp.roll(reversed_q[:, 0], 1, axis=1)
    own_pair = jnp.stack([zero_row, reversed_q[:, 1]], axis=1)
    partner = jnp.where(lax.axis_index("seq") == 0, own_pair, reversed_q[:, ::-1])
    first = jnp.stack([0.5 * (packed[0] + partner[0]), 0.5 * (packed[1] - partner[1])])
    second = jnp.stack([0.5 * (packed[1] + partner[1]), 0.5 * (partner[0] - packed[0])])
    return (first, second)


def inverse_rows(spectra):
    seq_count = lax.axis_size("seq")
    row_count = spectra.shape[2]
    period_len = 2 * row_count * seq_count
    inner_table = angle_table(row_count, row_count, row_count)
    cos_inner = jnp.cos(inner_table)
    sin_inner = jnp.sin(inner_table)
    real_sum = contract("qr,krw->kqw", cos_inner, spectra[0]) - contract(
        "qr,krw->kqw", sin_inner, spectra[1]
    )
    imag_sum = contract("qr,krw->kqw", cos_inner, spectra[1]) + contract(
        "qr,krw->kqw", sin_inner, spectra[0]
    )
    coarse = coarse_order(
        2 * lax.axis_index("seq") + lax.broadcasted_iota(jnp.int32, (2, row_count), 0), seq_count
    )
    position = lax.broadcasted_iota(jnp.int32, (2, row_count), 1)
    phases = angle_of(position * coarse, period_len)
    cos_turn = jnp.cos(phases)[:, :, None]
    sin_turn = jnp.sin(phases)[:, :, None]
    rotated = jnp.stack(
        [real_sum * cos_turn - imag_sum * sin_turn, real_sum * sin_turn + imag_sum * cos_turn]
    )
    target_grid = lax.broadcasted_iota(jnp.int32, (seq_count, 2 * seq_count), 0)
    slot_grid = lax.broadcasted_iota(jnp.int32, (seq_count, 2 * seq_count), 1)
    last_table = angle_of(target_grid * coarse_order(slot_grid, seq_count), 2 * seq_count)
    cos_last = jnp.cos(last_table)
    sin_last = jnp.sin(last_table)
    pieces = lax.all_to_all(rotated, "seq", split_axis=2, concat_axis=1, tiled=True)
    value = contract("sk,krw->srw", cos_last, pieces[0]) - contract(
        "sk,krw->srw", sin_last, pieces[1]
    )
    other = contract("sk,krw->srw", sin_last, pieces[0]) + contract(
        "sk,krw->srw", cos_last, pieces[1]
    )
    gathered = (value / period_len, other / period_len)
    gathered = jnp.concatenate([gathered[0], gathered[1]], axis=2)
    home_rows = lax.all_to_all(gathered, "seq", split_axis=0, concat_axis=1, tiled=True)
    return home_rows.reshape(row_count, home_rows.shape[2])


def invert_all(spectra):
    half_width = spectra.shape[3] // 2
    joined = jnp.stack(
        [
            spectra[0, :, :, :half_width] - spectra[1, :, :, half_width:],
            spectra[1, :, :, :half_width] + spectra[0, :, :, half_width:],
        ]
    )
    return inverse_rows(joined)


def shards(signal, grad_out, filter_taps, skip_gain):
    channels = filter_taps.shape[1]
    signal_rows = signal[0].astype(jnp.float32)
    grad_rows = grad_out[0].astype(jnp.float32)
    tap_half = filter_taps.shape[1] // 2
    columns = jnp.concatenate(
        [signal_rows, filter_taps[:, :tap_half], grad_rows, filter_taps[:, tap_half:]], axis=1
    )
    first, second = split_pairs(forward_spectra(columns))
    signal_spec = first[:, :, :, :channels]
    grad_spec = second[:, :, :, :channels]
    own_spec = jnp.concatenate([first[:, :, :, channels:], second[:, :, :, channels:]], axis=3)
    input_spec = jnp.stack(
        [
            grad_spec[0] * own_spec[0] + grad_spec[1] * own_spec[1],
            grad_spec[1] * own_spec[0] - grad_spec[0] * own_spec[1],
        ]
    )
    filter_terms = jnp.stack(
        [
            grad_spec[0] * signal_spec[0] + grad_spec[1] * signal_spec[1],
            grad_spec[1] * signal_spec[0] - grad_spec[0] * signal_spec[1],
        ]
    )
    shared_terms = summed_on_arrival(filter_terms, "batch", 3)
    rows_back = invert_all(jnp.concatenate([input_spec, shared_terms], axis=3))
    filter_grad = gather_directly(rows_back[:, channels:], "batch", 1)
    input_grad = (rows_back[:, :channels] + skip_gain[None, :] * grad_rows).astype(jnp.bfloat16)
    return (input_grad[None], filter_grad)


def solution(mesh):
    return jax.shard_map(
        shards,
        mesh=mesh,
        in_specs=(P("batch", "seq", None), P("batch", "seq", None), P("seq", None), P()),
        out_specs=(P("batch", "seq", None), P("seq", None)),
        check_vma=False,
    )
```

profile of v0, /device:TPU:1, one launch (start us, length us, event | category | flops | bytes accessed | tf_op | source)
XLA Modules:
  0.0 239.2 jit_solution(16720733413574259168)
XLA Ops:
  0.6 1.0 fusion.173
  1.6 1.0 bitcast_convert_fusion
  2.7 1.7 copy.29
  4.4 15.1 %all-to-all-start = ((f32[1,256,768]{2,0,1:T(1,128)}), f32[1,256,768]{2,0,1:T(1,128)S(1)}, u32[]{:S(2)}, u32[]{:S(2)}) async-start(f32[1,256,768]{2,0,1:T(1,128)} %copy.29), calls=%async_computation | async-start | bytes 1572864 | tf_op jit(solution)/shard_map/all_to_all | solution.py:65
  19.7 21.7 %all-to-all-done = f32[1,256,768]{2,0,1:T(1,128)S(1)} async-done(((f32[1,256,768]{2,0,1:T(1,128)}), f32[1,256,768]{2,0,1:T(1,128)S(1)}, u32[]{:S(2)}, u32[]{:S(2)}) %all-to-all-start) | async-done | bytes 786464 | tf_op jit(solution)/shard_map/all_to_all | solution.py:65
  41.4 1.9 reduce
  46.5 1.1 add_bitcast_fusion
  47.8 2.2 copy.32
  50.0 8.2 %all-to-all-start.1 = ((f32[2,128,4,384]{3,2,0,1:T(4,128)}), f32[2,128,4,384]{3,2,0,1:T(4,128)S(1)}, u32[]{:S(2)}, u32[]{:S(2)}) async-start(f32[2,128,4,384]{3,2,0,1:T(4,128)} %copy.32), calls=%async_computation.1 | async-start | bytes 3145728 | tf_op jit(solution)/shard_map/all_to_all | solution.py:99
  58.2 37.3 %all-to-all-done.1 = f32[2,128,4,384]{3,2,0,1:T(4,128)S(1)} async-done(((f32[2,128,4,384]{3,2,0,1:T(4,128)}), f32[2,128,4,384]{3,2,0,1:T(4,128)S(1)}, u32[]{:S(2)}, u32[]{:S(2)}) %all-to-all-start.1) | async-done | bytes 1572896 | tf_op jit(solution)/shard_map/all_to_all | solution.py:99
  97.4 1.8 fusion.35
  99.6 1.8 fusion.37
  101.4 1.8 convolution_add_fusion
  103.2 1.8 convolution_subtract_fusion
  105.0 1.3 fusion.4
  106.3 7.2 %slice.129 = f32[2,1,256,384]{2,3,0,1:T(8,128)} reverse(f32[2,1,256,384]{2,3,0,1:T(8,128)} %get-tuple-element.22), dimensions={2} | reverse | bytes 1572864 | tf_op jit(solution)/shard_map/slice | solution.py:111
  113.5 1.2 slice.158
  114.7 7.2 %slice.133 = f32[2,1,256,384]{2,3,1,0:T(8,128)} reverse(f32[2,1,256,384]{2,3,1,0:T(8,128)} %get-tuple-element.23), dimensions={2} | reverse | bytes 1572864 | tf_op jit(solution)/shard_map/slice | solution.py:112
  121.9 8.7 %rev.4 = f32[2,2,256,384]{2,3,1,0:T(8,128)} reverse(f32[2,2,256,384]{2,3,1,0:T(8,128)S(1)} %pad_maximum_fusion), dimensions={1,2} | reverse | bytes 3145728 | tf_op jit(solution)/shard_map/rev | solution.py:113
  130.6 1.5 maximum_bitcast_fusion.1
  132.3 1.3 maximum_select_fusion
  134.3 1.1 copy_bitcast_fusion.1
  135.4 8.5 %all-to-all-start.2 = ((f32[4,2,2,256,64]{3,4,2,1,0:T(8,128)}), f32[4,2,2,256,64]{3,4,2,1,0:T(8,128)S(1)}, u32[]{:S(2)}, u32[]{:S(2)}) async-start(f32[4,2,2,256,64]{3,4,2,1,0:T(8,128)} %copy_bitcast_fusion.1), calls=%async_computation.2 | async-start | bytes 2097152 | tf_op jit(solution)/shard_map/all_to_all | solution.py:15
  144.2 13.2 %all-to-all-done.2 = f32[4,2,2,256,64]{3,4,2,1,0:T(8,128)S(1)} async-done(((f32[4,2,2,256,64]{3,4,2,1,0:T(8,128)}), f32[4,2,2,256,64]{3,4,2,1,0:T(8,128)S(1)}, u32[]{:S(2)}, u32[]{:S(2)}) %all-to-all-start.2) | async-done | bytes 1048608 | tf_op jit(solution)/shard_map/all_to_all | solution.py:15
  157.6 1.4 fusion.31
  159.0 1.4 fusion.33
  160.4 1.4 convolution_add_fusion.2
  161.9 1.5 subtract_bitcast_fusion.1
  164.0 32.6 %all_to_all.61 = f32[2,2,256,160]{3,1,0,2:T(2,128)S(1)} all-to-all(f32[2,2,256,160]{3,1,0,2:T(2,128)S(1)} %copy.41), channel_id=1, replica_groups=mesh['batch'=4,'seq'=64] {'seq'}, dimensions={2} | all-to-all | bytes 1310720 | tf_op jit(solution)/shard_map/all_to_all | solution.py:147
  202.0 22.7 %all_to_all.62 = f32[64,4,320]{2,1,0:T(4,128)S(1)} all-to-all(f32[64,4,320]{2,1,0:T(4,128)S(1)} %copy.49), channel_id=1, replica_groups=mesh['batch'=4,'seq'=64] {'seq'}, dimensions={0} | all-to-all | bytes 655360 | tf_op jit(solution)/shard_map/all_to_all | solution.py:156
  225.6 7.7 %all-to-all-start.5 = ((f32[4,256,64]{1,2,0:T(8,128)}), f32[4,256,64]{1,2,0:T(8,128)S(1)}, u32[]{:S(2)}, u32[]{:S(2)}) async-start(f32[4,256,64]{1,2,0:T(8,128)} %broadcast_in_dim.5), calls=%async_computation.5 | async-start | bytes 524288 | tf_op jit(solution)/shard_map/all_to_all | solution.py:21
  234.0 4.3 %all-to-all-done.5 = f32[4,256,64]{1,2,0:T(8,128)S(1)} async-done(((f32[4,256,64]{1,2,0:T(8,128)}), f32[4,256,64]{1,2,0:T(8,128)S(1)}, u32[]{:S(2)}, u32[]{:S(2)}) %all-to-all-start.5) | async-done | bytes 262176 | tf_op jit(solution)/shard_map/all_to_all | solution.py:21
  (61 shorter events, 15.5 us)
Async XLA Ops:
  4.4 37.0 %all-to-all-start = ((f32[1,256,768]{2,0,1:T(1,128)}), f32[1,256,768]{2,0,1:T(1,128)S(1)}, u32[]{:S(2)}, u32[]{:S(2)}) async-start(f32[1,256,768]{2,0,1:T(1,128)} %copy.29), calls=%async_computation | async-start | bytes 1572864 | tf_op jit(solution)/shard_map/all_to_all | solution.py:65
  19.6 26.9 %copy-start.2 = (s32[128]{0:T(128)}, s32[128]{0:T(128)S(1)}, u32[]{:S(2)}) copy-start(s32[128]{0:T(128)S(1)} %get-tuple-element.44) | copy-start | bytes 1540
  19.6 26.9 %copy-start.4 = (s32[128]{0:T(128)}, s32[128]{0:T(128)S(1)}, u32[]{:S(2)}) copy-start(s32[128]{0:T(128)S(1)} %get-tuple-element.45) | copy-start | bytes 1540
  50.0 45.6 %all-to-all-start.1 = ((f32[2,128,4,384]{3,2,0,1:T(4,128)}), f32[2,128,4,384]{3,2,0,1:T(4,128)S(1)}, u32[]{:S(2)}, u32[]{:S(2)}) async-start(f32[2,128,4,384]{3,2,0,1:T(4,128)} %copy.32), calls=%async_computation.1 | async-start | bytes 3145728 | tf_op jit(solution)/shard_map/all_to_all | solution.py:99
  130.6 1.6 copy-start
  135.4 22.0 %all-to-all-start.2 = ((f32[4,2,2,256,64]{3,4,2,1,0:T(8,128)}), f32[4,2,2,256,64]{3,4,2,1,0:T(8,128)S(1)}, u32[]{:S(2)}, u32[]{:S(2)}) async-start(f32[4,2,2,256,64]{3,4,2,1,0:T(8,128)} %copy_bitcast_fusion.1), calls=%async_computation.2 | async-start | bytes 2097152 | tf_op jit(solution)/shard_map/all_to_all | solution.py:15
  197.0 0.8 copy-start.3
  197.0 0.8 copy-start.5
  202.0 31.3 %copy-start.1 = (bf16[1,256,256]{2,1,0:T(8,128)(2,1)S(1)}, bf16[1,256,256]{2,1,0:T(8,128)(2,1)}, u32[]{:S(2)}) copy-start(bf16[1,256,256]{2,1,0:T(8,128)(2,1)} %param.5) | copy-start | bytes 393220
  202.0 31.3 %copy-start.6 = (f32[256]{0:T(256)S(1)}, f32[256]{0:T(256)}, u32[]{:S(2)}) copy-start(f32[256]{0:T(256)} %param.7) | copy-start | bytes 3076
  225.6 12.7 %all-to-all-start.5 = ((f32[4,256,64]{1,2,0:T(8,128)}), f32[4,256,64]{1,2,0:T(8,128)S(1)}, u32[]{:S(2)}, u32[]{:S(2)}) async-start(f32[4,256,64]{1,2,0:T(8,128)} %broadcast_in_dim.5), calls=%async_computation.5 | async-start | bytes 524288 | tf_op jit(solution)/shard_map/all_to_all | solution.py:21
where the time goes:
time: 241 us; the launch traced here: 239 us
  waiting for transfers between devices  76.6 us (32%)
  blocking collectives  55.3 us (23%)
  starting transfers between devices  39.6 us (16%)
  local copies, waits for them, and re-layouts  36.1 us (15%)
  matrix products  20.2 us (8%)
  other arithmetic  10.4 us (4%)
    all_to_all x1, waiting for transfers between devices, forward_spectra(): lax.all_to_all(rotated, 'seq', split_axis=1, concat_axis=2, tiled=True)  37.3 us
    all_to_all x1, blocking collectives, inverse_rows(): lax.all_to_all(rotated, 'seq', split_axis=2, concat_axis=1, tiled=True)  32.6 us
    all_to_all x1, blocking collectives, inverse_rows(): lax.all_to_all(gathered, 'seq', split_axis=0, concat_axis=1, tiled=True)  22.7 us
    all_to_all x1, waiting for transfers between devices, forward_spectra(): lax.all_to_all(columns.reshape(1, row_count, columns.shape[1]), 'seq', sp...  21.7 us
    dot_general x16, matrix products, contract(): return jnp.einsum(form, table, operand, precision=lax.Precision.HIGHEST)  20.2 us
    all_to_all x1, starting transfers between devices, forward_spectra(): lax.all_to_all(columns.reshape(1, row_count, columns.shape[1]), 'seq', sp...  15.1 us
    all_to_all x1, waiting for transfers between devices, summed_on_arrival(): lax.all_to_all(parts, axis, split_axis=0, concat_axis=0, tiled=True)  13.2 us
    rev x1, local copies, waits for them, and re-layouts, split_pairs(): reversed_q[:, ::-1]  8.74 us
  transfers between devices with their start and end apart: 4, of which 4 were waited for; matrix products, arithmetic and copies ran while one was open for 0% of the time, Pallas kernels for 0%

commit v1 on v0

--- a/solution.py
+++ b/solution.py
@@ -62,12 +62,18 @@
     row_count = columns.shape[0]
     part_rows = row_count // seq_count
     period_len = 2 * row_count * seq_count
-    spread = lax.all_to_all(
-        columns.reshape(1, row_count, columns.shape[1]),
-        "seq",
-        split_axis=1,
-        concat_axis=0,
-        tiled=True,
+    spread = jnp.concatenate(
+        lax.all_to_all(
+            jnp.stack(
+                jnp.split(
+                    columns.reshape(1, row_count, columns.shape[1]), lax.axis_size("seq"), axis=1
+                )
+            ),
+            "seq",
+            0,
+            0,
+        ),
+        axis=0,
     )
     slot_grid = lax.broadcasted_iota(jnp.int32, (2 * seq_count, seq_count), 0)
     source_grid = lax.broadcasted_iota(jnp.int32, (2 * seq_count, seq_count), 1)

time: 241 us -> 275 us (1.14)
  local copies, waits for them, and re-layouts: 36.1 us -> 72.7 us
    unnamed x15 -> x78, local copies, waits for them, and re-layouts: 1 us -> 38.8 us
where the time goes in v1:
time: 275 us; the launch traced here: 274 us
  waiting for transfers between devices  76.6 us (28%)
  local copies, waits for them, and re-layouts  72.7 us (26%)
  blocking collectives  55.3 us (20%)
  starting transfers between devices  39.6 us (14%)
  matrix products  20.2 us (7%)
  other arithmetic  8.48 us (3%)
    unnamed x78, local copies, waits for them, and re-layouts  38.8 us
    all_to_all x1, waiting for transfers between devices, forward_spectra(): lax.all_to_all(rotated, 'seq', split_axis=1, concat_axis=2, tiled=True)  37.3 us
    all_to_all x1, blocking collectives, inverse_rows(): lax.all_to_all(rotated, 'seq', split_axis=2, concat_axis=1, tiled=True)  32.6 us
    all_to_all x1, blocking collectives, inverse_rows(): lax.all_to_all(gathered, 'seq', split_axis=0, concat_axis=1, tiled=True)  22.7 us
    all_to_all x1, waiting for transfers between devices, forward_spectra(): lax.all_to_all(jnp.stack(jnp.split(columns.reshape(1, row_count, columns....  21.7 us
    dot_general x16, matrix products, contract(): return jnp.einsum(form, table, operand, precision=lax.Precision.HIGHEST)  20.2 us
    all_to_all x1, starting transfers between devices, forward_spectra(): lax.all_to_all(jnp.stack(jnp.split(columns.reshape(1, row_count, columns....  15.1 us
    all_to_all x1, waiting for transfers between devices, summed_on_arrival(): lax.all_to_all(parts, axis, split_axis=0, concat_axis=0, tiled=True)  13.2 us
  transfers between devices with their start and end apart: 4, of which 4 were waited for; matrix products, arithmetic and copies ran while one was open for 0% of the time, Pallas kernels for 0%

profile of v1, /device:TPU:1, one launch (start us, length us, event | category | flops | bytes accessed | tf_op | source)
XLA Modules:
  0.0 273.9 jit_solution(12642059580337318563)
XLA Ops:
  0.6 1.0 fusion.172
  1.6 1.0 bitcast_convert_fusion
  41.1 15.1 %all-to-all-start = ((f32[64,1,4,768]{3,2,1,0:T(4,128)}), f32[64,1,4,768]{3,2,1,0:T(4,128)S(1)}, u32[]{:S(2)}, u32[]{:S(2)}) async-start(f32[64,1,4,768]{3,2,1,0:T(4,128)} %constant_dynamic-update-slice_fusion), calls=%async_computation | async-start | bytes 1572864 | tf_op jit(solution)/shard_map/all_to_all | solution.py:66
  56.4 21.7 %all-to-all-done = f32[64,1,4,768]{3,2,1,0:T(4,128)S(1)} async-done(((f32[64,1,4,768]{3,2,1,0:T(4,128)}), f32[64,1,4,768]{3,2,1,0:T(4,128)S(1)}, u32[]{:S(2)}, u32[]{:S(2)}) %all-to-all-start) | async-done | bytes 786464 | tf_op jit(solution)/shard_map/all_to_all | solution.py:66
  79.2 1.0 fusion.18
  80.2 1.0 convolution_subtract_fusion.1
  81.2 1.1 add_bitcast_fusion
  82.4 2.2 copy.29
  84.7 8.2 %all-to-all-start.1 = ((f32[2,128,4,384]{3,2,0,1:T(4,128)}), f32[2,128,4,384]{3,2,0,1:T(4,128)S(1)}, u32[]{:S(2)}, u32[]{:S(2)}) async-start(f32[2,128,4,384]{3,2,0,1:T(4,128)} %copy.29), calls=%async_computation.1 | async-start | bytes 3145728 | tf_op jit(solution)/shard_map/all_to_all | solution.py:105
  92.9 37.3 %all-to-all-done.1 = f32[2,128,4,384]{3,2,0,1:T(4,128)S(1)} async-done(((f32[2,128,4,384]{3,2,0,1:T(4,128)}), f32[2,128,4,384]{3,2,0,1:T(4,128)S(1)}, u32[]{:S(2)}, u32[]{:S(2)}) %all-to-all-start.1) | async-done | bytes 1572896 | tf_op jit(solution)/shard_map/all_to_all | solution.py:105
  132.1 1.8 fusion.35
  134.3 1.8 fusion.37
  136.1 1.8 convolution_add_fusion
  137.9 1.8 convolution_subtract_fusion
  139.7 1.3 fusion.4
  141.0 7.2 %slice.129 = f32[2,1,256,384]{2,3,0,1:T(8,128)} reverse(f32[2,1,256,384]{2,3,0,1:T(8,128)} %get-tuple-element.22), dimensions={2} | reverse | bytes 1572864 | tf_op jit(solution)/shard_map/slice | solution.py:117
  148.2 1.2 slice.158
  149.4 7.2 %slice.133 = f32[2,1,256,384]{2,3,1,0:T(8,128)} reverse(f32[2,1,256,384]{2,3,1,0:T(8,128)} %get-tuple-element.23), dimensions={2} | reverse | bytes 1572864 | tf_op jit(solution)/shard_map/slice | solution.py:118
  156.6 8.8 %rev.4 = f32[2,2,256,384]{2,3,1,0:T(8,128)} reverse(f32[2,2,256,384]{2,3,1,0:T(8,128)S(1)} %pad_maximum_fusion), dimensions={1,2} | reverse | bytes 3145728 | tf_op jit(solution)/shard_map/rev | solution.py:119
  165.4 1.5 maximum_bitcast_fusion.1
  167.0 1.3 maximum_select_fusion
  169.1 1.1 copy_bitcast_fusion.1
  170.2 8.5 %all-to-all-start.2 = ((f32[4,2,2,256,64]{3,4,2,1,0:T(8,128)}), f32[4,2,2,256,64]{3,4,2,1,0:T(8,128)S(1)}, u32[]{:S(2)}, u32[]{:S(2)}) async-start(f32[4,2,2,256,64]{3,4,2,1,0:T(8,128)} %copy_bitcast_fusion.1), calls=%async_computation.2 | async-start | bytes 2097152 | tf_op jit(solution)/shard_map/all_to_all | solution.py:15
  178.9 13.2 %all-to-all-done.2 = f32[4,2,2,256,64]{3,4,2,1,0:T(8,128)S(1)} async-done(((f32[4,2,2,256,64]{3,4,2,1,0:T(8,128)}), f32[4,2,2,256,64]{3,4,2,1,0:T(8,128)S(1)}, u32[]{:S(2)}, u32[]{:S(2)}) %all-to-all-start.2) | async-done | bytes 1048608 | tf_op jit(solution)/shard_map/all_to_all | solution.py:15
  192.3 1.4 fusion.31
  193.8 1.4 fusion.33
  195.2 1.4 convolution_add_fusion.2
  196.6 1.4 subtract_bitcast_fusion.1
  198.7 32.6 %all_to_all.54 = f32[2,2,256,160]{3,1,0,2:T(2,128)S(1)} all-to-all(f32[2,2,256,160]{3,1,0,2:T(2,128)S(1)} %copy.38), channel_id=1, replica_groups=mesh['batch'=4,'seq'=64] {'seq'}, dimensions={2} | all-to-all | bytes 1310720 | tf_op jit(solution)/shard_map/all_to_all | solution.py:153
  236.7 22.7 %all_to_all.55 = f32[64,4,320]{2,1,0:T(4,128)S(1)} all-to-all(f32[64,4,320]{2,1,0:T(4,128)S(1)} %copy.46), channel_id=1, replica_groups=mesh['batch'=4,'seq'=64] {'seq'}, dimensions={0} | all-to-all | bytes 655360 | tf_op jit(solution)/shard_map/all_to_all | solution.py:162
  260.4 7.7 %all-to-all-start.5 = ((f32[4,256,64]{1,2,0:T(8,128)}), f32[4,256,64]{1,2,0:T(8,128)S(1)}, u32[]{:S(2)}, u32[]{:S(2)}) async-start(f32[4,256,64]{1,2,0:T(8,128)} %broadcast_in_dim.5), calls=%async_computation.5 | async-start | bytes 524288 | tf_op jit(solution)/shard_map/all_to_all | solution.py:21
  268.7 4.3 %all-to-all-done.5 = f32[4,256,64]{1,2,0:T(8,128)S(1)} async-done(((f32[4,256,64]{1,2,0:T(8,128)}), f32[4,256,64]{1,2,0:T(8,128)S(1)}, u32[]{:S(2)}, u32[]{:S(2)}) %all-to-all-start.5) | async-done | bytes 262176 | tf_op jit(solution)/shard_map/all_to_all | solution.py:21
  (122 shorter events, 51.8 us)
Async XLA Ops:
  41.1 37.0 %all-to-all-start = ((f32[64,1,4,768]{3,2,1,0:T(4,128)}), f32[64,1,4,768]{3,2,1,0:T(4,128)S(1)}, u32[]{:S(2)}, u32[]{:S(2)}) async-start(f32[64,1,4,768]{3,2,1,0:T(4,128)} %constant_dynamic-update-slice_fusion), calls=%async_computation | async-start | bytes 1572864 | tf_op jit(solution)/shard_map/all_to_all | solution.py:66
  56.3 24.9 %copy-start.2 = (s32[128]{0:T(128)}, s32[128]{0:T(128)S(1)}, u32[]{:S(2)}) copy-start(s32[128]{0:T(128)S(1)} %get-tuple-element.42) | copy-start | bytes 1540
  56.3 24.9 %copy-start.4 = (s32[128]{0:T(128)}, s32[128]{0:T(128)S(1)}, u32[]{:S(2)}) copy-start(s32[128]{0:T(128)S(1)} %get-tuple-element.43) | copy-start | bytes 1540
  84.7 45.6 %all-to-all-start.1 = ((f32[2,128,4,384]{3,2,0,1:T(4,128)}), f32[2,128,4,384]{3,2,0,1:T(4,128)S(1)}, u32[]{:S(2)}, u32[]{:S(2)}) async-start(f32[2,128,4,384]{3,2,0,1:T(4,128)} %copy.29), calls=%async_computation.1 | async-start | bytes 3145728 | tf_op jit(solution)/shard_map/all_to_all | solution.py:105
  165.4 1.6 copy-start
  170.2 22.0 %all-to-all-start.2 = ((f32[4,2,2,256,64]{3,4,2,1,0:T(8,128)}), f32[4,2,2,256,64]{3,4,2,1,0:T(8,128)S(1)}, u32[]{:S(2)}, u32[]{:S(2)}) async-start(f32[4,2,2,256,64]{3,4,2,1,0:T(8,128)} %copy_bitcast_fusion.1), calls=%async_computation.2 | async-start | bytes 2097152 | tf_op jit(solution)/shard_map/all_to_all | solution.py:15
  231.7 0.8 copy-start.3
  231.7 0.8 copy-start.5
  236.7 31.4 %copy-start.1 = (bf16[1,256,256]{2,1,0:T(8,128)(2,1)S(1)}, bf16[1,256,256]{2,1,0:T(8,128)(2,1)}, u32[]{:S(2)}) copy-start(bf16[1,256,256]{2,1,0:T(8,128)(2,1)} %param.5) | copy-start | bytes 393220
  236.7 31.4 %copy-start.6 = (f32[256]{0:T(256)S(1)}, f32[256]{0:T(256)}, u32[]{:S(2)}) copy-start(f32[256]{0:T(256)} %param.7) | copy-start | bytes 3076
  260.4 12.7 %all-to-all-start.5 = ((f32[4,256,64]{1,2,0:T(8,128)}), f32[4,256,64]{1,2,0:T(8,128)S(1)}, u32[]{:S(2)}, u32[]{:S(2)}) async-start(f32[4,256,64]{1,2,0:T(8,128)} %broadcast_in_dim.5), calls=%async_computation.5 | async-start | bytes 524288 | tf_op jit(solution)/shard_map/all_to_all | solution.py:21
